TPU v7x, 256 devices: a whole 4x4x8 slice. The times are simulated.
256 devices in a mesh: row: 32 (over x, z_hi, y), col: 8 (over z_lo, core).
Axes of the slice: x: 4, y: 4, z: 8 (z_hi: 2, z_lo: 4; z = z_hi * 4 + z_lo), core: 2. Of those that a mesh axis runs over, the one named last changes fastest.
Arguments:
- lanczos_now: float32 [1, 256, 1024], P(None, 'row', 'col'), may hold values from -80 to 80, as said below
- lanczos_prev: float32 [1, 256, 1024], P(None, 'row', 'col'), may hold values from -6 to 6
- beta_prev: float32 [1], replicated, may hold values from 0.3 to 1.5
- valence_energy: float32 [256], P('row'), may hold values from -1.5 to -0.5
- conduction_energy: float32 [1024], P('col'), may hold values from 0.5 to 2.5
- valence_panel: float32 [16384, 256], P(('row', 'col')), may hold values from -0.375 to 0.375
- conduction_panel: float32 [16384, 1024], P(('row', 'col')), may hold values from -0.1875 to 0.1875
- screened_coulomb: float32 [16384, 16384], P('row', 'col'), may hold values from -0.046875 to 0.046875
- bare_coulomb: float32 [16384, 16384], P('row', 'col'), may hold values from -0.046875 to 0.046875
Outputs:
- lanczos_next: float32 [1, 256, 1024], P(None, 'row', 'col')
- coefficients: float32 [1, 2], replicated
Inputs may be any that keep to these rules, and one draw needn't show every extreme that they name: `lanczos_now`: real entries; the vectors of a chain are not normalized.
All inputs are finite; a program needn't handle non-finite values.
Results may differ from a plain program's by a relative error of at most 0.0002.
Values sent between devices are 32-bit elements; how exact they have to be, the bound alone decides.
A program may use at most 128 MiB of HBM per device.

v0:
```python
import jax
import jax.numpy as jnp
from jax import lax
from jax.sharding import Mesh
from jax.sharding import PartitionSpec as P

V = 256
C = 1024
COL = ("col_0", "col_1")
ROW = ("row_0", "row_1", "row_2")
ROW_COL = ("row_0", "row_1", "row_2", "col_0", "col_1")
precise = lax.Precision.HIGHEST
epsilon = 1e-06


def copy_for_each(shard, axis):
    copies = jnp.broadcast_to(shard, (lax.axis_size(axis), *shard.shape))
    return lax.all_to_all(copies, axis, split_axis=0, concat_axis=0, tiled=True)


def joined_along(parts, dim):
    dims = list(parts.shape[1:])
    dims[dim] *= parts.shape[0]
    return jnp.moveaxis(parts, 0, dim).reshape(dims)


def gather_directly(shard, axis, dim):
    parts = copy_for_each(shard, axis)
    return joined_along(parts, dim)


def sent_together(arrays, axis, dim, along):
    ends, at = ([], 0)
    for a in arrays[:-1]:
        at += a.shape[along]
        ends.append(at)
    both = jnp.concatenate(arrays, axis=along)
    return tuple(jnp.split(lax.all_gather(both, axis, axis=dim, tiled=True), ends, axis=along))


def split_up(shard, dim, count):
    before, after = (shard.shape[:dim], shard.shape[dim + 1 :])
    return jnp.moveaxis(shard.reshape(*before, count, -1, *after), dim, 0)


def sent_and_summed(shard, axis, dim):
    parts = split_up(shard, dim, lax.axis_size(axis))
    arrived = lax.all_to_all(parts, axis, split_axis=0, concat_axis=0, tiled=True)
    return arrived.sum(axis=0)


def side_by_side(arrays, axis, dim, along):
    columns = [a.reshape(*a.shape[:along], -1) for a in arrays]
    both = jnp.concatenate(columns, axis=along)
    out, at, done = (sent_and_summed(both, axis, dim), 0, [])
    for a, column in zip(arrays, columns):
        piece = out[..., at : at + column.shape[along]]
        done.append(piece.reshape(*piece.shape[:along], *a.shape[along:]))
        at += column.shape[along]
    return tuple(done)


def reduced_to_own(parts, axes, order):
    inside = parts.shape[1:]
    parts = parts.reshape(*(lax.axis_size(a) for a in axes), *inside)
    parts = jnp.moveaxis(parts, order, range(len(axes))).reshape(-1, *inside)
    for k in order:
        parts = lax.psum_scatter(parts, axes[k], scatter_dimension=0, tiled=True)
    return parts[0]


def sum_by_axis(shard, axes, order, dim):
    count = lax.axis_size(axes)
    return reduced_to_own(split_up(shard, dim, count), axes, order)


def one_axis_at_a_time(shard, axes):
    for axis in axes:
        shard = lax.psum(shard, axis)
    return shard


def per_device(
    lanczos_now,
    lanczos_prev,
    beta_prev,
    valence_energy,
    conduction_energy,
    valence_panel,
    conduction_panel,
    screened_coulomb,
    bare_coulomb,
):
    column_points = screened_coulomb.shape[1]
    wider = gather_directly(lanczos_now, COL, 2)
    vectors = lax.all_gather(wider, ROW, axis=1, tiled=True)
    products = jnp.einsum("pv,kvc->pkc", valence_panel, vectors, precision=precise)
    density = jnp.sum(products * conduction_panel[:, None, :], axis=2)
    pair_local = jnp.einsum("pc,kvc->pkv", conduction_panel, vectors, precision=precise)
    every_panel, every_density = sent_together((valence_panel, density), ROW_COL, 0, 1)
    first_point = lax.axis_index(COL) * column_points
    panel = lax.dynamic_slice_in_dim(every_panel, first_point, column_points, 0)
    far_density = lax.dynamic_slice_in_dim(every_density, first_point, column_points, 0)
    pair_terms = (
        jnp.einsum("mkv,nv->mkn", gather_directly(pair_local, COL, 0), panel, precision=precise)
        * screened_coulomb[:, None, :]
    )
    screened = jnp.einsum("mkn,nv->mkv", pair_terms, panel, precision=precise)
    potential = jnp.dot(bare_coulomb, far_density, precision=precise)
    direct_rows, local_potential = side_by_side((screened, potential), COL, 0, 2)
    weighted = local_potential[:, :, None] * conduction_panel[:, None, :]
    bare_term = jnp.einsum("pv,pkc->vkc", valence_panel, weighted, precision=precise)
    screened_term = jnp.einsum("mkv,mc->vkc", direct_rows, conduction_panel, precision=precise)
    band_rows = sum_by_axis(2.0 * bare_term - screened_term, ROW, (0, 2, 1), 0)
    kernel_part = sent_and_summed(band_rows, COL, 2)
    kernel_part = jnp.transpose(kernel_part, (1, 0, 2))
    gaps = conduction_energy[None, None, :] - valence_energy[None, :, None]
    image = gaps * lanczos_now + kernel_part
    inverse_size = 1.0 / (V * C)
    sum_qu, sum_qq, sum_uu, sum_up, sum_pp, sum_qp = (
        one_axis_at_a_time(jnp.sum(lanczos_now * image, axis=(1, 2)), ROW_COL),
        one_axis_at_a_time(jnp.sum(lanczos_now * lanczos_now, axis=(1, 2)), ROW_COL),
        one_axis_at_a_time(jnp.sum(image * image, axis=(1, 2)), ROW_COL),
        one_axis_at_a_time(jnp.sum(image * lanczos_prev, axis=(1, 2)), ROW_COL),
        one_axis_at_a_time(jnp.sum(lanczos_prev * lanczos_prev, axis=(1, 2)), ROW_COL),
        one_axis_at_a_time(jnp.sum(lanczos_now * lanczos_prev, axis=(1, 2)), ROW_COL),
    )
    coef_alpha = sum_qu * inverse_size / (sum_qq * inverse_size + epsilon)
    mean_ww = (
        sum_uu
        - 2.0 * coef_alpha * sum_qu
        - 2.0 * beta_prev * sum_up
        + coef_alpha * coef_alpha * sum_qq
        + beta_prev * beta_prev * sum_pp
        + 2.0 * coef_alpha * beta_prev * sum_qp
    ) * inverse_size
    resid = (
        image - coef_alpha[:, None, None] * lanczos_now - beta_prev[:, None, None] * lanczos_prev
    )
    beta_next = jnp.sqrt(mean_ww + epsilon)
    return (resid / beta_next[:, None, None], jnp.stack([coef_alpha, beta_next], axis=1))


def solution(mesh):
    torus = Mesh(mesh.devices.reshape(4, 2, 4, 4, 2), ("row_0", "row_1", "row_2", "col_0", "col_1"))
    return jax.shard_map(
        per_device,
        mesh=torus,
        in_specs=(
            P(None, ROW, COL),
            P(None, ROW, COL),
            P(),
            P(ROW),
            P(COL),
            P(ROW_COL, None),
            P(ROW_COL, None),
            P(ROW, COL),
            P(ROW, COL),
        ),
        out_specs=(P(None, ROW, COL), P()),
        check_vma=False,
    )
```

profile of v0, /device:TPU:1, one launch (start us, length us, event | category | flops | bytes accessed | tf_op | source)
XLA Modules:
  0.0 726.4 jit_solution(2510422371659446498)
XLA Ops:
  7.2 0.7 broadcast_in_dim.4
  7.9 12.2 %all_to_all.20 = f32[8,1,8,128]{3,2,1,0:T(8,128)} all-to-all(f32[8,1,8,128]{3,2,1,0:T(8,128)S(1)} %broadcast_in_dim.4), channel_id=1, replica_groups=mesh['row_0'=4,'row_1'=2,'row_2'=4,'col_0'=4,'col_1'=2] {'col_0','col_1'}, dimensions={0} | all-to-all | bytes 65536 | tf_op jit(solution)/shard_map/all_to_all | solution.py:18
  20.2 80.5 %all-gather.3.cloned.1.call-done = f32[1,256,1024]{2,1,0:T(8,128)} async-done(((f32[1,8,1024]{2,1,0:T(8,128)}), f32[1,256,1024]{2,1,0:T(8,128)}) %all-gather.3.cloned.1.call-update) | async-done | bytes 1048592 | tf_op jit(solution)/shard_map/all_gather | solution.py:96
  100.7 2.1 fusion.7
  103.0 1.5 pad_maximum_fusion.1
  104.5 2.4 fusion.9
  106.9 1.1 broadcast_in_dim.5
  108.0 5.7 all-to-all-start.1
  113.7 17.8 %all-to-all-done.1 = f32[8,64,1,256]{3,2,1,0:T(1,128)S(1)} async-done(((f32[8,64,1,256]{3,2,1,0:T(1,128)}), f32[8,64,1,256]{3,2,1,0:T(1,128)S(1)}, u32[]{:S(2)}, u32[]{:S(2)}) %all-to-all-start.1) | async-done | bytes 524320 | tf_op jit(solution)/shard_map/all_to_all | solution.py:18
  131.5 406.5 %all-gather.5.cloned.1.call-done = f32[16384,257]{1,0:T(8,128)} async-done(((f32[64,257]{1,0:T(8,128)}), f32[16384,257]{1,0:T(8,128)}) %all-gather.5.cloned.1.call-update) | async-done | bytes 16842768 | tf_op jit(solution)/shard_map/all_gather | solution.py:38
  538.1 3.4 slice-done
  541.8 0.9 copy-done.1
  542.6 3.4 convolution_bitcast_fusion.1
  546.0 6.5 split.8
  552.5 3.6 fusion.3
  556.1 3.5 fusion
  559.7 27.3 %all_to_all.21 = f32[8,64,1,257]{3,1,2,0:T(8,128)S(1)} all-to-all(f32[8,64,1,257]{3,1,2,0:T(8,128)S(1)} %pad_maximum_fusion), channel_id=1, replica_groups=mesh['row_0'=4,'row_1'=2,'row_2'=4,'col_0'=4,'col_1'=2] {'col_0','col_1'}, dimensions={0} | all-to-all | bytes 1052672 | tf_op jit(solution)/shard_map/all_to_all | solution.py:48
  587.2 1.1 fusion.5
  588.2 1.1 fusion.6
  589.3 1.1 copy.25
  590.5 19.3 %reduce-scatter.4.cloned.1.call-done = f32[8,8,1,1024]{3,1,0,2:T(8,128)} async-done(((f32[32,8,1,1024]{3,1,0,2:T(8,128)}), f32[8,8,1,1024]{3,1,0,2:T(8,128)}) %reduce-scatter.4.cloned.1.call-update) | async-done | bytes 262160 | tf_op jit(solution)/shard_map/reduce_scatter | solution.py:68
  609.8 24.6 %reduce-scatter.6.cloned.1.call-done = f32[2,8,1,1024]{3,1,0,2:T(8,128)} async-done(((f32[8,8,1,1024]{3,1,0,2:T(8,128)}), f32[2,8,1,1024]{3,1,0,2:T(8,128)}) %reduce-scatter.6.cloned.1.call-update) | async-done | bytes 65552 | tf_op jit(solution)/shard_map/reduce_scatter | solution.py:68
  634.5 24.0 %reduce-scatter.8.cloned.1.call-done = f32[1,8,1,1024]{3,1,0,2:T(8,128)} async-done(((f32[2,8,1,1024]{3,1,0,2:T(8,128)}), f32[1,8,1,1024]{3,1,0,2:T(8,128)}) %reduce-scatter.8.cloned.1.call-update) | async-done | bytes 32784 | tf_op jit(solution)/shard_map/reduce_scatter | solution.py:68
  658.4 3.7 all-to-all-start.3
  662.8 4.3 all-to-all-done.3
  667.2 0.8 multiply_reduce_fusion.2
  668.0 9.6 %all-reduce.2 = (f32[1]{0:T(128)}, f32[1]{0:T(128)}, f32[1]{0:T(128)}, f32[1]{0:T(128)}, f32[1]{0:T(128)}, /*index=5*/f32[1]{0:T(128)}) all-reduce(f32[1]{0:T(128)} %bitcast.30, f32[1]{0:T(128)} %bitcast.26, f32[1]{0:T(128)} %bitcast.27, f32[1]{0:T(128)} %bitcast.31, ...), channel_id=1, replica_groups=mesh['row_0'=4,'row_1'=2,'row_2'=4,'col_0'=4,'col_1'=2] {'row_0'}, use_global_device_ids=true, to_apply=%region_19.0 | all-reduce | flops 6 | bytes 48 | tf_op jit(solution)/shard_map/psum | solution.py:79
  677.5 8.4 %all-reduce.4 = (f32[1]{0:T(128)}, f32[1]{0:T(128)}, f32[1]{0:T(128)}, f32[1]{0:T(128)}, f32[1]{0:T(128)}, /*index=5*/f32[1]{0:T(128)}) all-reduce(f32[1]{0:T(128)} %get-tuple-element.20, f32[1]{0:T(128)} %get-tuple-element.21, f32[1]{0:T(128)} %get-tuple-element.22, ...), channel_id=1, replica_groups=mesh['row_0'=4,'row_1'=2,'row_2'=4,'col_0'=4,'col_1'=2] {'row_1'}, use_global_device_ids=true, to_apply=%region_20.0 | all-reduce | flops 6 | bytes 48 | tf_op jit(solution)/shard_map/psum | solution.py:79
  685.9 9.1 %all-reduce.1 = (f32[1]{0:T(128)}, f32[1]{0:T(128)}, f32[1]{0:T(128)}, f32[1]{0:T(128)}, f32[1]{0:T(128)}, /*index=5*/f32[1]{0:T(128)}) all-reduce(f32[1]{0:T(128)} %get-tuple-element.32, f32[1]{0:T(128)} %get-tuple-element.33, f32[1]{0:T(128)} %get-tuple-element.34, ...), channel_id=1, replica_groups=mesh['row_0'=4,'row_1'=2,'row_2'=4,'col_0'=4,'col_1'=2] {'row_2'}, use_global_device_ids=true, to_apply=%region_21.0 | all-reduce | flops 6 | bytes 48 | tf_op jit(solution)/shard_map/psum | solution.py:79
  695.1 7.8 %all-reduce = (f32[1]{0:T(128)}, f32[1]{0:T(128)}, f32[1]{0:T(128)}, f32[1]{0:T(128)}, f32[1]{0:T(128)}, /*index=5*/f32[1]{0:T(128)}) all-reduce(f32[1]{0:T(128)} %get-tuple-element.14, f32[1]{0:T(128)} %get-tuple-element.15, f32[1]{0:T(128)} %get-tuple-element.16, ...), channel_id=1, replica_groups=mesh['row_0'=4,'row_1'=2,'row_2'=4,'col_0'=4,'col_1'=2] {'col_0'}, use_global_device_ids=true, to_apply=%region_22.0 | all-reduce | flops 6 | bytes 48 | tf_op jit(solution)/shard_map/psum | solution.py:79
  702.9 10.7 %all-reduce.3 = (f32[1]{0:T(128)}, f32[1]{0:T(128)}, f32[1]{0:T(128)}, f32[1]{0:T(128)}, f32[1]{0:T(128)}, /*index=5*/f32[1]{0:T(128)}) all-reduce(f32[1]{0:T(128)} %get-tuple-element.8, f32[1]{0:T(128)} %get-tuple-element.9, f32[1]{0:T(128)} %get-tuple-element.10, ...), channel_id=1, replica_groups=mesh['row_0'=4,'row_1'=2,'row_2'=4,'col_0'=4,'col_1'=2] {'col_1'}, use_global_device_ids=true, to_apply=%region_23.0 | all-reduce | flops 6 | bytes 48 | tf_op jit(solution)/shard_map/psum | solution.py:79
  719.2 0.7 subtract_divide_fusion
  (34 shorter events, 1.6 us)
Async XLA Ops:
  7.2 93.6 %all-gather.3.cloned.1.call-start = ((), (), s32[]{:S(2)}) async-start(), calls=%async_computation.7 | async-start | bytes 1081344 | tf_op jit(solution)/shard_map/all_gather | solution.py:96
  20.2 517.9 %all-gather.5.cloned.1.call-start = ((), (), s32[]{:S(2)}) async-start(), calls=%async_computation.8 | async-start | bytes 25264128 | tf_op jit(solution)/shard_map/all_gather | solution.py:38
  108.0 23.5 %all-to-all-start.1 = ((f32[8,64,1,256]{3,2,1,0:T(1,128)}), f32[8,64,1,256]{3,2,1,0:T(1,128)S(1)}, u32[]{:S(2)}, u32[]{:S(2)}) async-start(f32[8,64,1,256]{3,2,1,0:T(1,128)} %broadcast_in_dim.5), calls=%async_computation.1 | async-start | bytes 1048576 | tf_op jit(solution)/shard_map/all_to_all | solution.py:18
  113.7 496.0 %reduce-scatter.4.cloned.1.call-start = ((), (), s32[]{:S(2)}) async-start(), calls=%async_computation.9 | async-start | bytes 1310720 | tf_op jit(solution)/shard_map/reduce_scatter | solution.py:68
  538.0 3.4 slice-start
  538.0 4.6 copy-start.1
  552.5 3.6 copy-start.2
  556.1 31.0 %copy-start.3 = (f32[64,256]{1,0:T(8,128)S(1)}, f32[64,256]{1,0:T(8,128)}, u32[]{:S(2)}) copy-start(f32[64,256]{1,0:T(8,128)} %param.14) | copy-start | bytes 196612
  559.6 27.6 %copy-start = (f32[64,1024]{1,0:T(8,128)S(1)}, f32[64,1024]{1,0:T(8,128)}, u32[]{:S(2)}) copy-start(f32[64,1024]{1,0:T(8,128)} %param.15) | copy-start | bytes 786436
  587.0 80.2 %copy-start.4 = (f32[1,8,128]{2,1,0:T(8,128)S(1)}, f32[1,8,128]{2,1,0:T(8,128)}, u32[]{:S(2)}) copy-start(f32[1,8,128]{2,1,0:T(8,128)} %param.9) | copy-start | bytes 12292
  587.0 80.2 %copy-start.5 = (f32[1,8,128]{2,1,0:T(8,128)S(1)}, f32[1,8,128]{2,1,0:T(8,128)}, u32[]{:S(2)}) copy-start(f32[1,8,128]{2,1,0:T(8,128)} %param.10) | copy-start | bytes 12292
  587.0 80.2 %copy-start.6 = (f32[8]{0:T(128)S(1)}, f32[8]{0:T(128)}, u32[]{:S(2)}) copy-start(f32[8]{0:T(128)} %param.12) | copy-start | bytes 100
  587.0 80.2 %copy-start.7 = (f32[128]{0:T(128)S(1)}, f32[128]{0:T(128)}, u32[]{:S(2)}) copy-start(f32[128]{0:T(128)} %param.13) | copy-start | bytes 1540
  590.4 44.0 %reduce-scatter.6.cloned.1.call-start = ((), (), s32[]{:S(2)}) async-start(), calls=%async_computation.10 | async-start | bytes 327680 | tf_op jit(solution)/shard_map/reduce_scatter | solution.py:68
  609.8 48.6 %reduce-scatter.8.cloned.1.call-start = ((), (), s32[]{:S(2)}) async-start(), calls=%async_computation.11 | async-start | bytes 98304 | tf_op jit(solution)/shard_map/reduce_scatter | solution.py:68
  658.4 8.7 %all-to-all-start.3 = ((f32[8,8,1,128]{3,1,2,0:T(8,128)}), f32[8,8,1,128]{3,1,2,0:T(8,128)S(1)}, u32[]{:S(2)}, u32[]{:S(2)}) async-start(f32[8,8,1,128]{3,1,2,0:T(8,128)} %bitcast.88), calls=%async_computation.6 | async-start | bytes 65536 | tf_op jit(solution)/shard_map/all_to_all | solution.py:48
Sparse Core Ops, SparseCore 0:
  20.3 80.3 all-gather.2
  104.6 433.3 all-gather.4
  590.5 19.1 reduce-scatter.3
  612.1 22.2 reduce-scatter.5
  636.7 21.6 reduce-scatter.7
where the time goes:
time: 727 us; the launch traced here: 726 us
  waiting for transfers between devices  577 us (79%)
  blocking collectives  85.2 us (12%)
  between operations  19.6 us (3%)
  matrix products  17 us (2%)
  local copies, waits for them, and re-layouts  14.3 us (2%)
  starting transfers between devices  9.62 us (1%)
    all_gather x1, waiting for transfers between devices, sent_together(): lax.all_gather(both, axis, axis=dim, tiled=True)  407 us
    all_gather x1, waiting for transfers between devices, per_device(): vectors = lax.all_gather(wider, ROW, axis=1, tiled=True)  80.5 us
    reduce_scatter x3, waiting for transfers between devices, reduced_to_own(): parts = lax.psum_scatter(parts, axes[k], scatter_dimension=0, tiled=True)  67.8 us
    psum x5, blocking collectives, one_axis_at_a_time(): shard = lax.psum(shard, axis)  45.6 us
    all_to_all x1, blocking collectives, sent_and_summed(): lax.all_to_all(parts, axis, split_axis=0, concat_axis=0, tiled=True)  27.3 us
    all_to_all x1, waiting for transfers between devices, copy_for_each(): return lax.all_to_all(copies, axis, split_axis=0, concat_axis=0, tiled=True)  17.8 us
  transfers between devices with their start and end apart: 7, of which 7 were waited for; matrix products, arithmetic and copies ran while one was open for 0% of the time, Pallas kernels for 0%

commit v1 on v0

--- a/solution.py
+++ b/solution.py
@@ -11,6 +11,12 @@
 ROW_COL = ("row_0", "row_1", "row_2", "col_0", "col_1")
 precise = lax.Precision.HIGHEST
 epsilon = 1e-06
+
+
+def add_all(array, mesh_axis):
+    parts = lax.all_gather(array, mesh_axis, axis=0, tiled=False)
+    total = parts.sum(axis=0)
+    return total
 
 
 def copy_for_each(shard, axis):
@@ -76,7 +82,7 @@
 
 def one_axis_at_a_time(shard, axes):
     for axis in axes:
-        shard = lax.psum(shard, axis)
+        shard = add_all(shard, axis)
     return shard
 
 

time: 727 us -> 785 us (1.080)
  local copies, waits for them, and re-layouts: 14.3 us -> 58.3 us
  other arithmetic: 3.62 us -> 21.6 us
    psum x5 -> x0, blocking collectives: 45.6 us -> none  [one_axis_at_a_time(): shard = lax.psum(shard, axis)]
    unnamed x17 -> x92, local copies, waits for them, and re-layouts: 0.93 us -> 44.9 us
    unnamed x0 -> x5, blocking collectives: none -> 42.1 us
    reduce_sum x0 -> x30, other arithmetic: none -> 18 us  [add_all(): total = parts.sum(axis=0)]
  transfers between devices with their start and end apart: 7 -> 7, of which waited for: 7 -> 7; matrix products, arithmetic and copies ran while one was open for 0% -> 1% of each run, Pallas kernels for 0% -> 0%
where the time goes in v1:
time: 785 us; the launch traced here: 784 us
  waiting for transfers between devices  576 us (73%)
  blocking collectives  81.6 us (10%)
  local copies, waits for them, and re-layouts  58.3 us (7%)
  other arithmetic  21.6 us (3%)
  between operations  20 us (3%)
  matrix products  17 us (2%)
  starting transfers between devices  9.62 us (1%)
    all_gather x1, waiting for transfers between devices, sent_together(): lax.all_gather(both, axis, axis=dim, tiled=True)  407 us
    all_gather x1, waiting for transfers between devices, per_device(): vectors = lax.all_gather(wider, ROW, axis=1, tiled=True)  80.5 us
    reduce_scatter x3, waiting for transfers between devices, reduced_to_own(): parts = lax.psum_scatter(parts, axes[k], scatter_dimension=0, tiled=True)  67.9 us
    unnamed x92, local copies, waits for them, and re-layouts  44.9 us
    unnamed x5, blocking collectives  42.1 us
    all_to_all x1, blocking collectives, sent_and_summed(): lax.all_to_all(parts, axis, split_axis=0, concat_axis=0, tiled=True)  27.3 us
    reduce_sum x30, other arithmetic, add_all(): total = parts.sum(axis=0)  18 us
    all_to_all x1, waiting for transfers between devices, copy_for_each(): return lax.all_to_all(copies, axis, split_axis=0, concat_axis=0, tiled=True)  17.8 us
  transfers between devices with their start and end apart: 7, of which 7 were waited for; matrix products, arithmetic and copies ran while one was open for 1% of the time, Pallas kernels for 0%

profile of v1, /device:TPU:1, one launch (start us, length us, event | category | flops | bytes accessed | tf_op | source)
XLA Modules:
  0.0 784.0 jit_solution(13575576369869841500)
XLA Ops:
  7.9 12.2 %all_to_all.20 = f32[8,1,8,128]{3,2,1,0:T(8,128)} all-to-all(f32[8,1,8,128]{3,2,1,0:T(8,128)S(1)} %broadcast_in_dim.4), channel_id=1, replica_groups=mesh['row_0'=4,'row_1'=2,'row_2'=4,'col_0'=4,'col_1'=2] {'col_0','col_1'}, dimensions={0} | all-to-all | bytes 65536 | tf_op jit(solution)/shard_map/all_to_all | solution.py:24
  20.2 80.5 %all-gather.3.cloned.1.call-done = f32[1,256,1024]{2,1,0:T(8,128)} async-done(((f32[1,8,1024]{2,1,0:T(8,128)}), f32[1,256,1024]{2,1,0:T(8,128)}) %all-gather.3.cloned.1.call-update) | async-done | bytes 1048592 | tf_op jit(solution)/shard_map/all_gather | solution.py:102
  100.7 2.1 fusion.7
  103.0 1.5 pad_maximum_fusion.1
  104.5 2.4 fusion.9
  108.0 5.7 all-to-all-start.1
  113.7 17.8 %all-to-all-done.1 = f32[8,64,1,256]{3,2,1,0:T(1,128)S(1)} async-done(((f32[8,64,1,256]{3,2,1,0:T(1,128)}), f32[8,64,1,256]{3,2,1,0:T(1,128)S(1)}, u32[]{:S(2)}, u32[]{:S(2)}) %all-to-all-start.1) | async-done | bytes 524320 | tf_op jit(solution)/shard_map/all_to_all | solution.py:24
  131.5 406.5 %all-gather.5.cloned.1.call-done = f32[16384,257]{1,0:T(8,128)} async-done(((f32[64,257]{1,0:T(8,128)}), f32[16384,257]{1,0:T(8,128)}) %all-gather.5.cloned.1.call-update) | async-done | bytes 16842768 | tf_op jit(solution)/shard_map/all_gather | solution.py:44
  538.1 3.4 slice-done
  542.6 3.4 convolution_bitcast_fusion.1
  546.0 6.5 split.8
  552.5 3.6 fusion.3
  556.1 3.5 fusion
  559.7 27.3 %all_to_all.21 = f32[8,64,1,257]{3,1,2,0:T(8,128)S(1)} all-to-all(f32[8,64,1,257]{3,1,2,0:T(8,128)S(1)} %pad_maximum_fusion), channel_id=1, replica_groups=mesh['row_0'=4,'row_1'=2,'row_2'=4,'col_0'=4,'col_1'=2] {'col_0','col_1'}, dimensions={0} | all-to-all | bytes 1052672 | tf_op jit(solution)/shard_map/all_to_all | solution.py:54
  590.5 19.3 %reduce-scatter.4.cloned.1.call-done = f32[8,8,1,1024]{3,1,0,2:T(8,128)} async-done(((f32[32,8,1,1024]{3,1,0,2:T(8,128)}), f32[8,8,1,1024]{3,1,0,2:T(8,128)}) %reduce-scatter.4.cloned.1.call-update) | async-done | bytes 262160 | tf_op jit(solution)/shard_map/reduce_scatter | solution.py:74
  609.9 24.6 %reduce-scatter.6.cloned.1.call-done = f32[2,8,1,1024]{3,1,0,2:T(8,128)} async-done(((f32[8,8,1,1024]{3,1,0,2:T(8,128)}), f32[2,8,1,1024]{3,1,0,2:T(8,128)}) %reduce-scatter.6.cloned.1.call-update) | async-done | bytes 65552 | tf_op jit(solution)/shard_map/reduce_scatter | solution.py:74
  634.5 24.0 %reduce-scatter.8.cloned.1.call-done = f32[1,8,1,1024]{3,1,0,2:T(8,128)} async-done(((f32[2,8,1,1024]{3,1,0,2:T(8,128)}), f32[1,8,1,1024]{3,1,0,2:T(8,128)}) %reduce-scatter.8.cloned.1.call-update) | async-done | bytes 32784 | tf_op jit(solution)/shard_map/reduce_scatter | solution.py:74
  658.5 3.7 all-to-all-start.3
  664.1 3.1 all-to-all-done.3
  672.1 1.4 dynamic-update-slice.15
  676.8 8.9 %all-reduce.32 = (f32[4]{0:T(128)S(1)}, f32[4]{0:T(128)S(1)}, f32[4]{0:T(128)S(1)}, f32[4]{0:T(128)S(1)}, f32[4]{0:T(128)S(1)}, /*index=5*/f32[4]{0:T(128)S(1)}) all-reduce(f32[4]{0:T(128)S(1)} %dynamic-update-slice.10, f32[4]{0:T(128)S(1)} %dynamic-update-slice, ...), channel_id=1, replica_groups=mesh['row_0'=4,'row_1'=2,'row_2'=4,'col_0'=4,'col_1'=2] {'row_0'}, use_global_device_ids=true, to_apply=%add.10 | all-reduce | flops 24 | bytes 192
  697.8 7.7 all-reduce.34
  706.6 1.4 dynamic-update-slice.12
  708.1 1.4 dynamic-update-slice.2
  710.1 1.4 dynamic-update-slice.7
  712.2 1.4 dynamic-update-slice.17
  714.2 1.4 dynamic-update-slice.22
  716.3 1.4 dynamic-update-slice.27
  718.3 8.5 %all-reduce.31 = (f32[4]{0:T(128)S(1)}, f32[4]{0:T(128)S(1)}, f32[4]{0:T(128)S(1)}, f32[4]{0:T(128)S(1)}, f32[4]{0:T(128)S(1)}, /*index=5*/f32[4]{0:T(128)S(1)}) all-reduce(f32[4]{0:T(128)S(1)} %dynamic-update-slice.12, f32[4]{0:T(128)S(1)} %dynamic-update-slice.2, ...), channel_id=1, replica_groups=mesh['row_0'=4,'row_1'=2,'row_2'=4,'col_0'=4,'col_1'=2] {'row_2'}, use_global_device_ids=true, to_apply=%add.12 | all-reduce | flops 24 | bytes 192
  729.4 1.4 dynamic-update-slice.3
  738.8 7.1 all-reduce.30
  757.4 9.9 %all-reduce.33 = (f32[2]{0:T(128)S(1)}, f32[2]{0:T(128)S(1)}, f32[2]{0:T(128)S(1)}, f32[2]{0:T(128)S(1)}, f32[2]{0:T(128)S(1)}, /*index=5*/f32[2]{0:T(128)S(1)}) all-reduce(f32[2]{0:T(128)S(1)} %dynamic-update-slice.14, f32[2]{0:T(128)S(1)} %dynamic-update-slice.4, ...), channel_id=1, replica_groups=mesh['row_0'=4,'row_1'=2,'row_2'=4,'col_0'=4,'col_1'=2] {'col_1'}, use_global_device_ids=true, to_apply=%add.14 | all-reduce | flops 12 | bytes 96
  (139 shorter events, 59.4 us)
Async XLA Ops:
  7.2 93.6 %all-gather.3.cloned.1.call-start = ((), (), s32[]{:S(2)}) async-start(), calls=%async_computation.7 | async-start | bytes 1081344 | tf_op jit(solution)/shard_map/all_gather | solution.py:102
  20.2 517.9 %all-gather.5.cloned.1.call-start = ((), (), s32[]{:S(2)}) async-start(), calls=%async_computation.8 | async-start | bytes 25264128 | tf_op jit(solution)/shard_map/all_gather | solution.py:44
  108.0 23.5 %all-to-all-start.1 = ((f32[8,64,1,256]{3,2,1,0:T(1,128)}), f32[8,64,1,256]{3,2,1,0:T(1,128)S(1)}, u32[]{:S(2)}, u32[]{:S(2)}) async-start(f32[8,64,1,256]{3,2,1,0:T(1,128)} %broadcast_in_dim.5), calls=%async_computation.1 | async-start | bytes 1048576 | tf_op jit(solution)/shard_map/all_to_all | solution.py:24
  113.7 496.1 %reduce-scatter.4.cloned.1.call-start = ((), (), s32[]{:S(2)}) async-start(), calls=%async_computation.9 | async-start | bytes 1310720 | tf_op jit(solution)/shard_map/reduce_scatter | solution.py:74
  538.0 3.4 slice-start
  538.0 4.6 copy-start.1
  552.5 3.6 copy-start.2
  556.1 31.1 %copy-start.3 = (f32[64,256]{1,0:T(8,128)S(1)}, f32[64,256]{1,0:T(8,128)}, u32[]{:S(2)}) copy-start(f32[64,256]{1,0:T(8,128)} %param.14) | copy-start | bytes 196612
  559.6 27.6 %copy-start = (f32[64,1024]{1,0:T(8,128)S(1)}, f32[64,1024]{1,0:T(8,128)}, u32[]{:S(2)}) copy-start(f32[64,1024]{1,0:T(8,128)} %param.15) | copy-start | bytes 786436
  587.0 75.3 %copy-start.12 = (u32[256]{0:T(256)S(1)}, u32[256]{0:T(256)}, u32[]{:S(2)}) copy-start(u32[256]{0:T(256)} %constant.33) | copy-start | bytes 3076
  587.0 75.9 %copy-start.11 = (u32[256]{0:T(256)S(1)}, u32[256]{0:T(256)}, u32[]{:S(2)}) copy-start(u32[256]{0:T(256)} %constant.38) | copy-start | bytes 3076
  587.0 76.4 %copy-start.10 = (u32[256]{0:T(256)S(1)}, u32[256]{0:T(256)}, u32[]{:S(2)}) copy-start(u32[256]{0:T(256)} %constant.43) | copy-start | bytes 3076
  587.0 80.3 %copy-start.4 = (f32[1,8,128]{2,1,0:T(8,128)S(1)}, f32[1,8,128]{2,1,0:T(8,128)}, u32[]{:S(2)}) copy-start(f32[1,8,128]{2,1,0:T(8,128)} %param.9) | copy-start | bytes 12292
  587.0 80.3 %copy-start.5 = (f32[1,8,128]{2,1,0:T(8,128)S(1)}, f32[1,8,128]{2,1,0:T(8,128)}, u32[]{:S(2)}) copy-start(f32[1,8,128]{2,1,0:T(8,128)} %param.10) | copy-start | bytes 12292
  587.0 80.3 %copy-start.6 = (f32[8]{0:T(128)S(1)}, f32[8]{0:T(128)}, u32[]{:S(2)}) copy-start(f32[8]{0:T(128)} %param.12) | copy-start | bytes 100
  587.0 80.3 %copy-start.7 = (f32[128]{0:T(128)S(1)}, f32[128]{0:T(128)}, u32[]{:S(2)}) copy-start(f32[128]{0:T(128)} %param.13) | copy-start | bytes 1540
  587.0 89.2 %copy-start.9 = (u32[256]{0:T(256)S(1)}, u32[256]{0:T(256)}, u32[]{:S(2)}) copy-start(u32[256]{0:T(256)} %constant.48) | copy-start | bytes 3076
  587.0 110.1 %copy-start.8 = (u32[256]{0:T(256)S(1)}, u32[256]{0:T(256)}, u32[]{:S(2)}) copy-start(u32[256]{0:T(256)} %constant.53) | copy-start | bytes 3076
  590.5 44.0 %reduce-scatter.6.cloned.1.call-start = ((), (), s32[]{:S(2)}) async-start(), calls=%async_computation.10 | async-start | bytes 327680 | tf_op jit(solution)/shard_map/reduce_scatter | solution.py:74
  609.8 48.7 %reduce-scatter.8.cloned.1.call-start = ((), (), s32[]{:S(2)}) async-start(), calls=%async_computation.11 | async-start | bytes 98304 | tf_op jit(solution)/shard_map/reduce_scatter | solution.py:74
  658.5 8.7 %all-to-all-start.3 = ((f32[8,8,1,128]{3,1,2,0:T(8,128)}), f32[8,8,1,128]{3,1,2,0:T(8,128)S(1)}, u32[]{:S(2)}, u32[]{:S(2)}) async-start(f32[8,8,1,128]{3,1,2,0:T(8,128)} %bitcast.123), calls=%async_computation.6 | async-start | bytes 65536 | tf_op jit(solution)/shard_map/all_to_all | solution.py:54
Sparse Core Ops, SparseCore 0:
  20.3 80.3 all-gather.2
  104.6 433.3 all-gather.4
  590.6 19.1 reduce-scatter.3
  612.2 22.2 reduce-scatter.5
  636.8 21.6 reduce-scatter.7
